TPU v7x, 64 devices: a 2x2x8 block of a 4x4x8 slice. The times are simulated.
64 devices in a mesh: rep: 8 (over x, y, core), dp: 8 (over z).
Axes of the slice: x: 2, y: 2, z: 8, core: 2. Of those that a mesh axis runs over, the one named last changes fastest.
The devices are a block of a 4x4x8 slice.
Arguments:
- x: bfloat16 [64, 2048, 640], P(('rep', 'dp')), parts along dimension 0
- dy: bfloat16 [64, 2048, 640], P(('rep', 'dp')), parts along dimension 0
- w_gate: bfloat16 [2, 640, 2048], replicated
- w_up: bfloat16 [2, 640, 2048], replicated
- w_down: bfloat16 [2, 2048, 640], replicated
- m_w_gate: float32 [2, 640, 2048], P(None, 'dp')
- m_w_up: float32 [2, 640, 2048], P(None, 'dp')
- m_w_down: float32 [2, 2048, 640], P(None, 'dp')
- v_w_gate: float32 [2, 640, 2048], P(None, 'dp')
- v_w_up: float32 [2, 640, 2048], P(None, 'dp')
- v_w_down: float32 [2, 2048, 640], P(None, 'dp')
Outputs:
- output 1: bfloat16 [16, 640, 2048], P('rep'), parts along dimension 0
- output 2: bfloat16 [16, 640, 2048], P('rep'), parts along dimension 0
- output 3: bfloat16 [16, 2048, 640], P('rep'), parts along dimension 0
- output 4: float32 [16, 640, 2048], P('rep', 'dp'), parts along dimension 0
- output 5: float32 [16, 640, 2048], P('rep', 'dp'), parts along dimension 0
- output 6: float32 [16, 2048, 640], P('rep', 'dp'), parts along dimension 0
- output 7: float32 [16, 640, 2048], P('rep', 'dp'), parts along dimension 0
- output 8: float32 [16, 640, 2048], P('rep', 'dp'), parts along dimension 0
- output 9: float32 [16, 2048, 640], P('rep', 'dp'), parts along dimension 0
There are 8 independent parts. A program takes and returns all parts, laid end to end along the dimension named above; an argument that names none is the same for every part.
All inputs are finite; a program needn't handle non-finite values.
Results may differ from a plain program's by a relative error of at most 0.022.
Values are sent between devices in bfloat16 or wider.
A program may use at most 768 MiB of HBM per device.

v0:
```python
import jax
import jax.numpy as jnp
from jax import lax

NAMES = ("w_gate", "w_up", "w_down")


def matmul(a, w):
    return jnp.dot(a, w, preferred_element_type=jnp.float32).astype(jnp.bfloat16)


def normed(h):
    wide = h.astype(jnp.float32)
    scale = lax.rsqrt(jnp.mean(wide**2, -1, keepdims=True) + 1e-6)
    return (wide * scale).astype(jnp.bfloat16)


def layer(h, w):
    a = normed(h)
    gate = jnp.dot(a, w["w_gate"], preferred_element_type=jnp.float32)
    up = jnp.dot(a, w["w_up"], preferred_element_type=jnp.float32)
    return h + matmul((jax.nn.silu(gate) * up).astype(jnp.bfloat16), w["w_down"])


def adamw(w, m, v, g):
    m = 0.9 * m + 0.1 * g
    v = 0.95 * v + 0.05 * g * g
    step = m * lax.rsqrt(v + 1e-8) + 0.1 * w
    return (w - 0.02 * step).astype(jnp.bfloat16), m, v


def stack(weights, h):
    for number in range(weights["w_gate"].shape[0]):
        h = layer(h, {name: w[number] for name, w in weights.items()})
    return h


def solution(mesh):
    groups = mesh.shape["rep"]

    def step(x, dy, *arrays):
        weights, m, v = (arrays[i : i + 3] for i in (0, 3, 6))
        x, dy = (t.reshape(groups, -1, *t.shape[1:]) for t in (x, dy))

        def of_a_group(x, dy):
            _, back = jax.vjp(lambda w: stack(w, x), dict(zip(NAMES, weights, strict=True)))
            by_weights = back(dy)[0]
            gradients = [by_weights[name].astype(jnp.float32) for name in NAMES]
            new = [adamw(w.astype(jnp.float32), m, v, g) for w, m, v, g in zip(weights, m, v, gradients, strict=True)]
            return tuple(one[which] for which in range(3) for one in new)

        return tuple(t.reshape(-1, *t.shape[2:]) for t in jax.vmap(of_a_group)(x, dy))

    return step
```

profile of v0, /device:TPU:30, one launch (start us, length us, event | category | flops | bytes accessed | tf_op | source)
XLA Modules:
  0.0 685.5 jit_solution(16006297199222951391)
XLA Ops:
  7.3 2.5 fusion.35
  9.7 4.4 copy
  14.2 8.5 %fusion.76 = f32[2048,2048]{1,0:T(8,128)S(1)} fusion(bf16[2,640,2048]{2,1,0:T(8,128)(2,1)} %param, bf16[1,2048,640]{2,1,0:T(8,128)(2,1)S(1)} %copy-done.1, f32[2048]{0:T(1024)S(1)} %add_rsqrt_fusion), kind=kOutput, calls=%fused_computation.88 | convolution fusion | flops 5372641280 | bytes 22028288 | tf_op jit(solution)/vmap(jvp())/dot_general | solution.py:20
  22.7 13.6 %fusion.74 = f32[2048,2048]{1,0:T(8,128)} fusion(bf16[2,640,2048]{2,1,0:T(8,128)(2,1)} %param.3, bf16[1,2048,640]{2,1,0:T(8,128)(2,1)S(1)} %copy-done.1, f32[2048]{0:T(1024)S(1)} %add_rsqrt_fusion), kind=kOutput, calls=%fused_computation.86 | convolution fusion | flops 5372641280 | bytes 22028288 | tf_op jit(solution)/vmap(jvp())/dot_general | solution.py:21
  36.3 8.6 %fusion.26 = bf16[2048,2048]{1,0:T(8,128)(2,1)S(1)} fusion(f32[2048,2048]{1,0:T(8,128)} %fusion.74, f32[2048,2048]{1,0:T(8,128)S(1)} %fusion.76), kind=kLoop, calls=%fused_computation.39 | loop fusion | flops 25165824 | bytes 41943040
  45.0 10.1 %fusion.39 = (f32[2048]{0:T(1024)S(1)}, bf16[1,1,2048,640]{2,3,1,0:T(8,128)(2,1)S(1)}) fusion(bf16[2048,2048]{1,0:T(8,128)(2,1)S(1)} %fusion.26, bf16[2,2048,640]{2,1,0:T(8,128)(2,1)} %param.4, bf16[1,2048,640]{1,2,0:T(8,128)(2,1)S(1)} %copy-done.11), kind=kOutput, calls=%fused_computation.56 | convolution fusion | flops 5375260672 | bytes 16261120 | tf_op jit(solution)/vmap(jvp())/dot_general | solution.py:9
  55.1 12.9 %fusion.64 = f32[2048,2048]{1,0:T(8,128)} fusion(bf16[2,640,2048]{2,1,0:T(8,128)(2,1)} %param, bf16[1,1,2048,640]{2,3,1,0:T(8,128)(2,1)S(1)} %get-tuple-element.10, f32[2048]{0:T(1024)S(1)} %bitcast.345), kind=kOutput, calls=%fused_computation.76 | convolution fusion | flops 5372641280 | bytes 22028288 | tf_op jit(solution)/vmap(jvp())/dot_general | solution.py:20
  68.0 12.1 %fusion.67 = f32[2048,2048]{1,0:T(8,128)} fusion(bf16[2,640,2048]{2,1,0:T(8,128)(2,1)} %param.3, bf16[1,1,2048,640]{2,3,1,0:T(8,128)(2,1)S(1)} %get-tuple-element.10, f32[2048]{0:T(1024)S(1)} %bitcast.346), kind=kOutput, calls=%fused_computation.79 | convolution fusion | flops 5372641280 | bytes 22028288 | tf_op jit(solution)/vmap(jvp())/dot_general | solution.py:21
  80.1 16.1 %fusion.42 = f32[1,2048,640]{2,1,0:T(8,128)} fusion(f32[2048,2048]{1,0:T(8,128)} %fusion.67, f32[2048,2048]{1,0:T(8,128)} %fusion.64, bf16[1,2048,640]{2,1,0:T(8,128)(2,1)S(1)} %copy-done.10), kind=kOutput, calls=%fused_computation.61 | convolution fusion | flops 5393874944 | bytes 41418752 | tf_op jit(solution)/vmap(transpose(jvp()))/dot_general | solution.py:9
  96.3 9.4 %convolution_convert_fusion.1 = bf16[2048,2048]{1,0:T(8,128)(2,1)S(1)} fusion(bf16[1,2048,640]{2,1,0:T(8,128)(2,1)S(1)} %copy-done.10, bf16[2,2048,640]{2,1,0:T(8,128)(2,1)} %param.4), kind=kOutput, calls=%fused_computation.48 | convolution fusion | flops 5372903424 | bytes 13631488 | tf_op jit(solution)/vmap(transpose(jvp()))/dot_general | solution.py:9
  105.8 3.2 copy-done.3
  109.0 15.8 %fusion.6 = bf16[2048,2048]{1,0:T(8,128)(2,1)} fusion(f32[2048,2048]{1,0:T(8,128)} %fusion.64, f32[2048,2048]{1,0:T(8,128)} %fusion.67, bf16[2048,2048]{1,0:T(8,128)(2,1)S(1)} %convolution_convert_fusion.1), kind=kLoop, calls=%fused_computation.11 | loop fusion | flops 50331648 | bytes 50331648
  124.8 3.0 copy.1
  127.8 13.2 %fusion.54 = bf16[2048,640]{0,1:T(8,128)(2,1)} fusion(bf16[2048,2048]{1,0:T(8,128)(2,1)} %copy-done.3, f32[2048,2048]{1,0:T(8,128)} %fusion.64, bf16[2,640,2048]{2,1,0:T(8,128)(2,1)} %param.3), kind=kOutput, calls=%fused_computation.66 | convolution fusion | flops 5395185664 | bytes 30408704 | tf_op jit(solution)/vmap(transpose(jvp()))/dot_general | solution.py:21
  141.0 8.2 %fusion.41 = (f32[2048]{0:T(1024)S(1)}, bf16[2048,640]{0,1:T(8,128)(2,1)S(1)}) fusion(bf16[1,1,2048,640]{2,3,1,0:T(8,128)(2,1)S(1)} %copy-done.7, bf16[2048,640]{0,1:T(8,128)(2,1)} %fusion.54, bf16[2048,2048]{1,0:T(8,128)(2,1)S(1)} %copy-done.4, bf16[2,640,2048]{2,1,0:T(8,128)(2,1)} %param), kind=kOutput, calls=%fused_computation.58 | convolution fusion | flops 5375260672 | bytes 18882560 | tf_op jit(solution)/vmap(transpose(jvp()))/dot_general | solution.py:20
  149.3 1.8 fusion.61
  151.1 1.5 copy-done.9
  152.5 11.0 %convolution_bitcast_fusion.1 = f32[1,2048,640]{2,1,0:T(8,128)} fusion(bf16[2048,2048]{1,0:T(8,128)(2,1)} %copy-done.2, bf16[2048,640]{0,1:T(8,128)(2,1)S(1)} %fusion.61), kind=kOutput, calls=%fused_computation.65 | convolution fusion | flops 5368709120 | bytes 16252928 | tf_op jit(solution)/vmap(transpose(jvp()))/dot_general | solution.py:9
  163.6 0.1 reduce-scatter.19.cloned.1.call-start
  163.7 1.6 copy-done.8
  165.3 9.4 %convolution_bitcast_fusion = f32[1,640,2048]{2,1,0:T(8,128)} fusion(bf16[2048,2048]{1,0:T(8,128)(2,1)} %fusion.6, bf16[1,1,2048,640]{2,3,1,0:T(8,128)(2,1)S(1)} %copy-done.8, f32[2048]{0:T(1024)S(1)} %bitcast.348), kind=kOutput, calls=%fused_computation.60 | convolution fusion | flops 5372641280 | bytes 16261120 | tf_op jit(solution)/vmap(transpose(jvp()))/dot_general | solution.py:20
  174.9 11.2 %convolution_convert_fusion = bf16[2048,2048]{1,0:T(8,128)(2,1)} fusion(bf16[2048,640]{0,1:T(8,128)(2,1)} %copy-done.9, bf16[2,2048,640]{2,1,0:T(8,128)(2,1)} %param.4), kind=kOutput, calls=%fused_computation.47 | convolution fusion | flops 5372903424 | bytes 13631488 | tf_op jit(solution)/vmap(transpose(jvp()))/dot_general | solution.py:9
  186.1 20.7 %fusion.48 = f32[1,640,2048]{2,1,0:T(8,128)} fusion(f32[2048,2048]{1,0:T(8,128)} %copy-done, f32[2048,2048]{1,0:T(8,128)} %fusion.74, bf16[2048,2048]{1,0:T(8,128)(2,1)} %convolution_convert_fusion, bf16[1,2048,640]{1,2,0:T(8,128)(2,1)} %copy, f32[2048]{0:T(1024)S(1)} %copy-done.18), kind=kOutput, calls=%fused_computation.63 | convolution fusion | flops 5418778624 | bytes 49815552 | tf_op jit(solution)/vmap(transpose(jvp()))/dot_general | solution.py:20
  206.9 12.8 %fusion.45 = f32[1,640,2048]{2,1,0:T(8,128)} fusion(bf16[2048,2048]{1,0:T(8,128)(2,1)} %copy-done.3, f32[2048,2048]{1,0:T(8,128)} %fusion.64, bf16[1,1,2048,640]{2,3,1,0:T(8,128)(2,1)S(1)} %copy-done.8, f32[2048]{0:T(1024)S(1)} %bitcast.349), kind=kOutput, calls=%fused_computation.62 | convolution fusion | flops 5397807104 | bytes 33038336 | tf_op jit(solution)/vmap(transpose(jvp()))/dot_general | solution.py:21
  219.9 1.6 copy-done.12
  221.5 13.1 %fusion.51 = f32[1,640,2048]{2,1,0:T(8,128)} fusion(bf16[2048,2048]{1,0:T(8,128)(2,1)} %convolution_convert_fusion, f32[2048,2048]{1,0:T(8,128)} %copy-done, bf16[1,2048,640]{1,2,0:T(8,128)(2,1)S(1)} %copy-done.12, f32[2048]{0:T(1024)S(1)} %copy-done.18), kind=kOutput, calls=%fused_computation.64 | convolution fusion | flops 5397807104 | bytes 33038336 | tf_op jit(solution)/vmap(transpose(jvp()))/dot_general | solution.py:21
  234.7 0.5 copy-done.19
  235.2 0.6 dynamic-slice
  236.4 1.1 convert_bitcast_fusion.4
  237.6 1.1 convert_bitcast_fusion.3
  238.8 3.5 fusion.124
  242.3 0.1 all-gather.10.cloned.1.call-start
  242.4 50.3 %reduce-scatter.19.cloned.1.call-done = f32[1,80,2048]{2,1,0:T(8,128)} async-done(((f32[1,640,2048]{2,1,0:T(8,128)}), f32[1,80,2048]{2,1,0:T(8,128)}) %reduce-scatter.19.cloned.1.call-update) | async-done | bytes 655376
  292.7 1.1 convert_bitcast_fusion.8
  293.8 62.3 %reduce-scatter.21.cloned.1.call-done = f32[1,80,2048]{2,1,0:T(8,128)} async-done(((f32[1,640,2048]{2,1,0:T(8,128)}), f32[1,80,2048]{2,1,0:T(8,128)}) %reduce-scatter.21.cloned.1.call-update) | async-done | bytes 655376
  356.1 1.1 convert_bitcast_fusion.7
  357.3 4.3 fusion.126
  361.7 57.2 %reduce-scatter.23.cloned.1.call-done = f32[1,80,2048]{2,1,0:T(8,128)} async-done(((f32[1,640,2048]{2,1,0:T(8,128)}), f32[1,80,2048]{2,1,0:T(8,128)}) %reduce-scatter.23.cloned.1.call-update) | async-done | bytes 655376
  418.9 1.1 convert_bitcast_fusion.6
  420.1 62.3 %reduce-scatter.25.cloned.1.call-done = f32[1,80,2048]{2,1,0:T(8,128)} async-done(((f32[1,640,2048]{2,1,0:T(8,128)}), f32[1,80,2048]{2,1,0:T(8,128)}) %reduce-scatter.25.cloned.1.call-update) | async-done | bytes 655376
  482.3 1.1 convert_bitcast_fusion.5
  483.5 3.5 fusion.125
  487.0 56.7 %all-gather.14.cloned.1.call-done = bf16[1,2,2048,640]{3,2,1,0:T(8,128)(2,1)} async-done(((bf16[1,2,256,640]{3,2,1,0:T(8,128)(2,1)}), bf16[1,2,2048,640]{3,2,1,0:T(8,128)(2,1)}) %all-gather.14.cloned.1.call-update) | async-done | bytes 5242896 | tf_op jit(solution)/reshape | solution.py:52
  543.8 62.0 %all-gather.10.cloned.1.call-done = bf16[1,2,640,2048]{3,2,1,0:T(8,128)(2,1)} async-done(((bf16[1,2,80,2048]{3,2,1,0:T(8,128)(2,1)}), bf16[1,2,640,2048]{3,2,1,0:T(8,128)(2,1)}) %all-gather.10.cloned.1.call-update) | async-done | bytes 5242896 | tf_op jit(solution)/reshape | solution.py:52
  605.7 62.0 %all-gather.12.cloned.1.call-done = bf16[1,2,640,2048]{3,2,1,0:T(8,128)(2,1)} async-done(((bf16[1,2,80,2048]{3,2,1,0:T(8,128)(2,1)}), bf16[1,2,640,2048]{3,2,1,0:T(8,128)(2,1)}) %all-gather.12.cloned.1.call-update) | async-done | bytes 5242896 | tf_op jit(solution)/reshape | solution.py:52
  667.7 6.2 copy.5
  673.9 2.4 copy.6
  676.3 2.4 copy.7
  (62 shorter events, 1.1 us)
Async XLA Ops:
  7.2 6.9 %copy-start.1 = (bf16[1,2048,640]{2,1,0:T(8,128)(2,1)S(1)}, bf16[1,2048,640]{2,1,0:T(8,128)(2,1)}, u32[]{:S(2)}) copy-start(bf16[1,2048,640]{2,1,0:T(8,128)(2,1)} %param.2) | copy-start | bytes 7864324
  7.2 229.2 %reduce-scatter.27.cloned.1.call-start = ((), (), s32[]{:S(2)}) async-start(), calls=%async_computation.13 | async-start | bytes 5898240
  14.1 8.6 %copy-start.17 = (f32[2048]{0:T(1024)}, f32[2048]{0:T(1024)S(1)}, u32[]{:S(2)}) copy-start(f32[2048]{0:T(1024)S(1)} %add_rsqrt_fusion) | copy-start | bytes 24580
  22.7 13.6 %copy-start = (f32[2048,2048]{1,0:T(8,128)}, f32[2048,2048]{1,0:T(8,128)S(1)}, u32[]{:S(2)}) copy-start(f32[2048,2048]{1,0:T(8,128)S(1)} %fusion.76) | copy-start | bytes 50331652
  36.3 8.6 %copy-start.11 = (bf16[1,2048,640]{1,2,0:T(8,128)(2,1)S(1)}, bf16[1,2048,640]{1,2,0:T(8,128)(2,1)}, u32[]{:S(2)}) copy-start(bf16[1,2048,640]{1,2,0:T(8,128)(2,1)} %copy) | copy-start | bytes 7864324
  44.9 10.1 %copy-start.2 = (bf16[2048,2048]{1,0:T(8,128)(2,1)}, bf16[2048,2048]{1,0:T(8,128)(2,1)S(1)}, u32[]{:S(2)}) copy-start(bf16[2048,2048]{1,0:T(8,128)(2,1)S(1)} %fusion.26) | copy-start | bytes 25165828
  55.0 12.9 %copy-start.6 = (bf16[1,1,2048,640]{2,3,1,0:T(8,128)(2,1)}, bf16[1,1,2048,640]{2,3,1,0:T(8,128)(2,1)S(1)}, u32[]{:S(2)}) copy-start(bf16[1,1,2048,640]{2,3,1,0:T(8,128)(2,1)S(1)} %get-tuple-element.10) | copy-start | bytes 7864324
  68.0 12.1 %copy-start.10 = (bf16[1,2048,640]{2,1,0:T(8,128)(2,1)S(1)}, bf16[1,2048,640]{2,1,0:T(8,128)(2,1)}, u32[]{:S(2)}) copy-start(bf16[1,2048,640]{2,1,0:T(8,128)(2,1)} %param.5) | copy-start | bytes 7864324
  96.3 141.3 %reduce-scatter.29.cloned.1.call-start = ((), (), s32[]{:S(2)}) async-start(), calls=%async_computation.14 | async-start | bytes 5898240
  105.8 3.2 copy-start.3
  127.8 13.2 %copy-start.4 = (bf16[2048,2048]{1,0:T(8,128)(2,1)S(1)}, bf16[2048,2048]{1,0:T(8,128)(2,1)}, u32[]{:S(2)}) copy-start(bf16[2048,2048]{1,0:T(8,128)(2,1)} %fusion.6) | copy-start | bytes 25165828
  127.8 13.2 %copy-start.7 = (bf16[1,1,2048,640]{2,3,1,0:T(8,128)(2,1)S(1)}, bf16[1,1,2048,640]{2,3,1,0:T(8,128)(2,1)}, u32[]{:S(2)}) copy-start(bf16[1,1,2048,640]{2,3,1,0:T(8,128)(2,1)} %copy-done.6) | copy-start | bytes 7864324
  151.1 1.5 copy-start.9
  163.5 1.7 copy-start.8
  163.6 129.1 %reduce-scatter.19.cloned.1.call-start = ((), (), s32[]{:S(2)}) async-start(), calls=%async_computation.9 | async-start | bytes 5898240
  174.8 11.3 %copy-start.18 = (f32[2048]{0:T(1024)S(1)}, f32[2048]{0:T(1024)}, u32[]{:S(2)}) copy-start(f32[2048]{0:T(1024)} %copy-done.17) | copy-start | bytes 24580
  174.8 181.3 %reduce-scatter.21.cloned.1.call-start = ((), (), s32[]{:S(2)}) async-start(), calls=%async_computation.10 | async-start | bytes 5898240
  206.8 212.1 %reduce-scatter.23.cloned.1.call-start = ((), (), s32[]{:S(2)}) async-start(), calls=%async_computation.11 | async-start | bytes 5898240
  219.7 1.7 copy-start.12
  219.8 262.5 %reduce-scatter.25.cloned.1.call-start = ((), (), s32[]{:S(2)}) async-start(), calls=%async_computation.12 | async-start | bytes 5898240
  234.5 0.7 copy-start.19
  234.5 4.2 copy-start.13
  234.5 4.2 copy-start.14
  234.6 309.2 %all-gather.14.cloned.1.call-start = ((), (), s32[]{:S(2)}) async-start(), calls=%async_computation.8 | async-start | bytes 5898240 | tf_op jit(solution)/reshape | solution.py:52
  242.3 363.4 %all-gather.10.cloned.1.call-start = ((), (), s32[]{:S(2)}) async-start(), calls=%async_computation.6 | async-start | bytes 5898240 | tf_op jit(solution)/reshape | solution.py:52
  293.8 189.6 %copy-start.15 = (f32[2,80,2048]{2,1,0:T(8,128)S(1)}, f32[2,80,2048]{2,1,0:T(8,128)}, u32[]{:S(2)}) copy-start(f32[2,80,2048]{2,1,0:T(8,128)} %param.8) | copy-start | bytes 3932164
  293.8 189.6 %copy-start.16 = (f32[2,80,2048]{2,1,0:T(8,128)S(1)}, f32[2,80,2048]{2,1,0:T(8,128)}, u32[]{:S(2)}) copy-start(f32[2,80,2048]{2,1,0:T(8,128)} %param.7) | copy-start | bytes 3932164
  361.6 306.1 %all-gather.12.cloned.1.call-start = ((), (), s32[]{:S(2)}) async-start(), calls=%async_computation.7 | async-start | bytes 5898240 | tf_op jit(solution)/reshape | solution.py:52
  667.7 6.2 copy-start.5
  667.7 8.5 %slice-start = ((s8[5242880]{0:T(1024)(128)(4,1)}), s8[4194304]{0:T(1024)(128)(4,1)S(1)}, s32[]{:S(2)}) async-start(s8[5242880]{0:T(1024)(128)(4,1)} %bitcast.337), calls=%async_computation.15 | async-start | bytes 8388608
  673.9 2.4 slice-start.1
Sparse Core Ops, SparseCore 0:
  96.4 65.3 reduce-scatter.26
  164.1 64.9 reduce-scatter.28
  232.1 60.5 reduce-scatter.18
  295.5 60.6 reduce-scatter.20
  358.3 60.5 reduce-scatter.22
  421.7 60.5 reduce-scatter.24
  483.9 59.8 all-gather.13
  545.9 59.7 all-gather.9
  607.9 59.7 all-gather.11
where the time goes:
time: 696 us; the launch traced here: 686 us
  waiting for transfers between devices  413 us (59%)
  matrix products  182 us (26%)
  other arithmetic  46.8 us (7%)
  local copies, waits for them, and re-layouts  27.3 us (4%)
  between operations  15.2 us (2%)
    unnamed x15, waiting for transfers between devices  233 us
    reshape x3, waiting for transfers between devices, step(): t.reshape(-1, *t.shape[2:])  181 us
    dot_general x5, matrix products, layer(): up = jnp.dot(a, w['w_up'], preferred_element_type=jnp.float32)  64.8 us
    dot_general x5, matrix products, layer(): gate = jnp.dot(a, w['w_gate'], preferred_element_type=jnp.float32)  59.8 us
    dot_general x5, matrix products, matmul(): jnp.dot(a, w, preferred_element_type=jnp.float32).astype(jnp.bfloat16)  57.8 us
    unnamed x49, local copies, waits for them, and re-layouts  26.7 us
    unnamed x4, other arithmetic  26.2 us
  transfers between devices with their start and end apart: 9, of which 7 were waited for; matrix products, arithmetic and copies ran while one was open for 22% of the time, Pallas kernels for 0%

commit v1 on v0

v1 whole, which is shorter than its diff:
```python
import functools

import jax
import jax.numpy as jnp
from jax import lax
from jax.experimental import pallas as pl
from jax.experimental.pallas import tpu as pltpu
from jax.sharding import PartitionSpec as P

MESH = pl.DeviceIdType.MESH
F32, BF16 = jnp.float32, jnp.bfloat16


def dot(a, b, ca, cb):
    return lax.dot_general(a, b, (((ca,), (cb,)), ((), ())), preferred_element_type=F32)


def normed(h):
    wide = h.astype(F32)
    scale = lax.rsqrt(jnp.mean(wide**2, -1, keepdims=True) + 1e-6)
    return (wide * scale).astype(BF16), scale


def norm_back(h, scale, da):
    wide, da = h.astype(F32), da.astype(F32)
    mean = jnp.mean(da * wide, -1, keepdims=True)
    return (da * scale - wide * (scale * scale * scale * mean)).astype(BF16)


def mlp(a, wg, wu):
    return dot(a, wg, 1, 0), dot(a, wu, 1, 0)


def mlp_back(gate, up, dh):
    s = jax.nn.sigmoid(gate)
    silu = gate * s
    dh = dh.astype(F32)
    return (dh * up * (s * (1 + gate * (1 - s)))).astype(BF16), (dh * silu).astype(BF16)


def adamw(w, m, v, g):
    m = 0.9 * m + 0.1 * g
    v = 0.95 * v + 0.05 * g * g
    step = m * lax.rsqrt(v + 1e-8) + 0.1 * w
    return (w - 0.02 * step).astype(BF16), m, v


def gather_kernel(n, layers, *refs):
    ins, outs, (send_sem, recv_sem, own_sem) = refs[:3], refs[3:6], refs[6:]
    me = lax.axis_index("dp")
    right, left = lax.rem(me + 1, n), lax.rem(me + n - 1, n)

    barrier = pltpu.get_barrier_semaphore()
    for neighbour in (left, right):
        pl.semaphore_signal(barrier, inc=1, device_id={"dp": neighbour}, device_id_type=MESH)
    pl.semaphore_wait(barrier, 2)

    items = [(k, layer) for layer in reversed(range(layers)) for k in (2, 0, 1)]

    def half(ref, k, layer, owner, way):
        rows, columns = ins[k].shape[1:]
        if columns % 256 == 0 and k < 2:
            return ref.at[layer, pl.ds(owner * rows, rows), pl.ds(way * (columns // 2), columns // 2)]
        return ref.at[layer, pl.ds(owner * rows + way * (rows // 2), rows // 2), :]

    def copy(i, way, hop):
        k, layer = items[i]
        owner = lax.rem(me + n - hop, n) if way == 0 else lax.rem(me + hop, n)
        src = half(ins[k], k, layer, 0, way) if hop == 0 else half(outs[k], k, layer, owner, way)
        return pltpu.make_async_remote_copy(
            src_ref=src,
            dst_ref=half(outs[k], k, layer, owner, way),
            send_sem=send_sem.at[i, way, hop],
            recv_sem=recv_sem.at[i, way, hop],
            device_id={"dp": right if way == 0 else left},
            device_id_type=MESH,
        )

    mine = []
    for i, (k, layer) in enumerate(items):
        for way in range(2):
            copy(i, way, 0).start()
    for i, (k, layer) in enumerate(items):
        rows = ins[k].shape[1]
        own = pltpu.make_async_copy(ins[k].at[layer], outs[k].at[layer, pl.ds(me * rows, rows), :], own_sem.at[i])
        own.start()
        mine.append(own)
    for hop in range(1, n):
        for i in range(len(items)):
            for way in range(2):
                copy(i, way, hop - 1).wait_recv()
                if hop < n - 1:
                    copy(i, way, hop).start()
    for hop in range(n - 1):
        for i in range(len(items)):
            for way in range(2):
                copy(i, way, hop).wait_send()
    for own in mine:
        own.wait()


def gather(n, blocks):
    layers = blocks[0].shape[0]
    outs = tuple(jax.ShapeDtypeStruct((b.shape[0], b.shape[1] * n, b.shape[2]), b.dtype) for b in blocks)
    vmem = pl.BlockSpec(memory_space=pltpu.VMEM)
    return pl.pallas_call(
        functools.partial(gather_kernel, n, layers),
        out_shape=outs,
        in_specs=[vmem] * 3,
        out_specs=(vmem,) * 3,
        scratch_shapes=[
            pltpu.SemaphoreType.DMA((3 * layers, 2, n - 1)),
            pltpu.SemaphoreType.DMA((3 * layers, 2, n - 1)),
            pltpu.SemaphoreType.DMA((3 * layers,)),
        ],
        compiler_params=pltpu.CompilerParams(collective_id=0, has_side_effects=True, vmem_limit_bytes=40 * 2**20),
    )(*blocks)


def solution(mesh):
    n = mesh.shape["dp"]

    def step(x, dy, *arrays):
        weights, ms, vs = (arrays[i : i + 3] for i in (0, 3, 6))
        x, dy = x[0], dy[0]
        wg, wu, wd = weights
        layers = wg.shape[0]
        saved, h = [], x
        for l in range(layers):
            a, scale = normed(h)
            gate, up = mlp(a, wg[l], wu[l])
            hid = (jax.nn.silu(gate) * up).astype(BF16)
            saved.append((h, a, scale, gate, up, hid))
            if l < layers - 1:
                h = h + dot(hid, wd[l], 1, 0).astype(BF16)
        grads = [[None] * layers for _ in range(3)]

        def reduced(g):
            return lax.psum_scatter(g.astype(BF16), "dp", scatter_dimension=0, tiled=True)

        d = dy
        for l in reversed(range(layers)):
            h, a, scale, gate, up, hid = saved[l]
            grads[2][l] = reduced(dot(hid, d, 0, 0))
            dh = dot(d, wd[l], 1, 1).astype(BF16)
            dgate, dup = mlp_back(gate, up, dh)
            grads[0][l] = reduced(dot(a, dgate, 0, 0))
            grads[1][l] = reduced(dot(a, dup, 0, 0))
            if l:
                da = dot(dgate, wg[l], 1, 1).astype(BF16) + dot(dup, wu[l], 1, 1).astype(BF16)
                d = d + norm_back(h, scale, da)
        me = lax.axis_index("dp")
        new = []
        for w, m, v, g in zip(weights, ms, vs, grads, strict=True):
            g = jnp.stack([t.astype(F32) for t in g])
            own = lax.dynamic_slice_in_dim(w, me * m.shape[1], m.shape[1], 1).astype(F32)
            new.append(adamw(own, m, v, g))
        full = gather(n, [one[0] for one in new])
        return (*full, *(one[1] for one in new), *(one[2] for one in new))

    seq, whole, rows = P(("rep", "dp")), P(), P(None, "dp")
    out_w, out_m = P("rep"), P("rep", "dp")
    return jax.shard_map(
        step,
        mesh=mesh,
        in_specs=(seq, seq, *[whole] * 3, *[rows] * 6),
        out_specs=(*[out_w] * 3, *[out_m] * 6),
        check_vma=False,
    )
```

time: 696 us -> 582 us (0.84)
  waiting for transfers between devices: 413 us -> 180 us
  Pallas kernels: 0 us -> 151 us
  other arithmetic: 46.8 us -> 14.2 us
    unnamed x15 -> x6, waiting for transfers between devices: 233 us -> 0.32 us
    reshape x3 -> x0, waiting for transfers between devices: 181 us -> none  [step(): t.reshape(-1, *t.shape[2:])]
    reduce_scatter x0 -> x6, waiting for transfers between devices: none -> 179 us  [reduced(): lax.psum_scatter(g.astype(BF16), 'dp', scatter_dimension=0, tiled=True)]
    pallas_call x0 -> x1, Pallas kernels: none -> 151 us  [gather(): pl.pallas_call(functools.partial(gather_kernel, n, layers), out_shape=out...]
    unnamed x4 -> x2, other arithmetic: 26.2 us -> 0.01 us
    convert_element_type x0 -> x3, other arithmetic: none -> 11.8 us  [adamw(): return ((w - 0.02 * step).astype(BF16), m, v)]
    reshape x3 -> x0, other arithmetic: 11.3 us -> none  [step(): t.reshape(-1, *t.shape[2:])]
    unnamed x49 -> x41, local copies, waits for them, and re-layouts: 26.7 us -> 26.5 us
  transfers between devices with their start and end apart: 9 -> 6, of which waited for: 7 -> 5; matrix products, arithmetic and copies ran while one was open for 22% -> 13% of each run, Pallas kernels for 0% -> 0%
where the time goes in v1:
time: 582 us; the launch traced here: 575 us
  matrix products  188 us (32%)
  waiting for transfers between devices  180 us (31%)
  Pallas kernels  151 us (26%)
  local copies, waits for them, and re-layouts  26.5 us (5%)
  between operations  14.8 us (3%)
  other arithmetic  14.2 us (2%)
    dot_general x15, matrix products, dot(): lax.dot_general(a, b, (((ca,), (cb,)), ((), ())), preferred_element_type=...  188 us
    reduce_scatter x6, waiting for transfers between devices, reduced(): lax.psum_scatter(g.astype(BF16), 'dp', scatter_dimension=0, tiled=True)  179 us
    pallas_call x1, Pallas kernels, gather(): pl.pallas_call(functools.partial(gather_kernel, n, layers), out_shape=out...  151 us
    unnamed x41, local copies, waits for them, and re-layouts  26.5 us
    convert_element_type x3, other arithmetic, adamw(): return ((w - 0.02 * step).astype(BF16), m, v)  11.8 us
  transfers between devices with their start and end apart: 6, of which 5 were waited for; matrix products, arithmetic and copies ran while one was open for 13% of the time, Pallas kernels for 0%

profile of v1, /device:TPU:30, one launch (start us, length us, event | category | flops | bytes accessed | tf_op | source)
XLA Modules:
  0.0 574.6 jit_solution(11387503032468535092)
XLA Ops:
  7.2 0.1 reduce-scatter.11.cloned.1.call-start
  7.3 3.0 copy.20
  10.3 0.6 fusion.13
  10.8 2.1 copy-done.7
  13.0 11.6 %fusion.43 = f32[2048,2048]{1,0:T(8,128)} fusion(bf16[2,640,2048]{2,1,0:T(8,128)(2,1)} %param.13, bf16[1,2048,640]{2,1,0:T(8,128)(2,1)S(1)} %copy-done.7, f32[2048]{0:T(1024)S(1)} %add_rsqrt_fusion.1), kind=kOutput, calls=%fused_computation.59 | convolution fusion | flops 5372641280 | bytes 22028288 | tf_op jit(solution)/shard_map/dot_general | solution.py:15
  24.5 16.7 %multiply_convert_fusion.1 = (bf16[2048,2048]{1,0:T(8,128)(2,1)}, f32[2048,2048]{1,0:T(8,128)}) fusion(f32[2048,2048]{1,0:T(8,128)} %fusion.43, bf16[2,640,2048]{2,1,0:T(8,128)(2,1)} %param.14, bf16[1,2048,640]{2,1,0:T(8,128)(2,1)} %param.11, f32[2048]{0:T(1024)S(1)} %add_rsqrt_fusion.1), kind=kOutput, calls=%fused_computation.13 | convolution fusion | flops 5397807104 | bytes 47194112 | tf_op jit(solution)/shard_map/dot_general | solution.py:15
  41.2 9.2 %fusion.17 = (f32[2048]{0:T(1024)S(1)}, bf16[2048,640]{0,1:T(8,128)(2,1)S(1)}) fusion(bf16[2048,2048]{1,0:T(8,128)(2,1)} %get-tuple-element.26, bf16[2,2048,640]{2,1,0:T(8,128)(2,1)} %param.15, bf16[1,2048,640]{1,2,0:T(8,128)(2,1)S(1)} %copy.20), kind=kOutput, calls=%fused_computation.32 | convolution fusion | flops 5375260672 | bytes 16261120 | tf_op jit(solution)/shard_map/dot_general | solution.py:15
  50.4 12.9 %fusion.37 = f32[2048,2048]{1,0:T(8,128)} fusion(bf16[2,640,2048]{2,1,0:T(8,128)(2,1)} %param.14, bf16[2048,640]{0,1:T(8,128)(2,1)S(1)} %get-tuple-element.29, f32[2048]{0:T(1024)S(1)} %add_rsqrt_fusion), kind=kOutput, calls=%fused_computation.53 | convolution fusion | flops 5372641280 | bytes 22028288 | tf_op jit(solution)/shard_map/dot_general | solution.py:15
  63.3 12.0 %fusion.34 = f32[2048,2048]{1,0:T(8,128)} fusion(bf16[2,640,2048]{2,1,0:T(8,128)(2,1)} %param.13, bf16[2048,640]{0,1:T(8,128)(2,1)S(1)} %get-tuple-element.29, f32[2048]{0:T(1024)S(1)} %add_rsqrt_fusion), kind=kOutput, calls=%fused_computation.50 | convolution fusion | flops 5372641280 | bytes 22028288 | tf_op jit(solution)/shard_map/dot_general | solution.py:15
  75.2 3.0 copy.21
  78.2 24.2 %fusion.2 = (bf16[2048,2048]{1,0:T(8,128)(2,1)}, bf16[2048,2048]{1,0:T(8,128)(2,1)}) fusion(f32[2048,2048]{1,0:T(8,128)} %fusion.34, f32[2048,2048]{1,0:T(8,128)} %fusion.37, bf16[2,2048,640]{2,1,0:T(8,128)(2,1)} %param.15, bf16[1,2048,640]{2,1,0:T(8,128)(2,1)} %param.12), kind=kOutput, calls=%fused_computation.6 | convolution fusion | flops 5431623680 | bytes 55574528 | tf_op jit(solution)/shard_map/dot_general | solution.py:15
  102.4 10.0 %convolution_convert_fusion.5 = bf16[2048,640]{0,1:T(8,128)(2,1)S(1)} fusion(bf16[2048,2048]{1,0:T(8,128)(2,1)} %get-tuple-element.24, bf16[2,640,2048]{2,1,0:T(8,128)(2,1)} %param.14), kind=kOutput, calls=%fused_computation.42 | convolution fusion | flops 5370019840 | bytes 13631488 | tf_op jit(solution)/shard_map/dot_general | solution.py:15
  112.4 7.8 %fusion.19 = (f32[2048]{0:T(1024)S(1)}, bf16[2048,640]{0,1:T(8,128)(2,1)S(1)}) fusion(bf16[2048,640]{0,1:T(8,128)(2,1)S(1)} %copy-done.3, bf16[2048,640]{0,1:T(8,128)(2,1)S(1)} %convolution_convert_fusion.5, bf16[2048,2048]{1,0:T(8,128)(2,1)S(1)} %copy-done.13, bf16[2,640,2048]{2,1,0:T(8,128)(2,1)} %param.13), kind=kOutput, calls=%fused_computation.34 | convolution fusion | flops 5376571392 | bytes 18882560 | tf_op jit(solution)/shard_map/dot_general | solution.py:15
  120.3 1.8 fusion.30
  122.1 1.5 copy-done.5
  123.6 7.1 %convolution_convert_fusion = bf16[2048,2048]{1,0:T(8,128)(2,1)S(1)} fusion(bf16[2048,640]{0,1:T(8,128)(2,1)S(1)} %fusion.30, bf16[2,2048,640]{2,1,0:T(8,128)(2,1)S(1)} %bitcast.81), kind=kOutput, calls=%fused_computation.23 | convolution fusion | flops 5372903424 | bytes 13631488 | tf_op jit(solution)/shard_map/dot_general | solution.py:15
  130.7 3.2 copy-done.12
  133.9 11.2 %fusion.23 = bf16[640,2048]{1,0:T(8,128)(2,1)} fusion(bf16[2048,2048]{1,0:T(8,128)(2,1)S(1)} %convolution_convert_fusion, f32[2048,2048]{1,0:T(8,128)} %fusion.43, bf16[1,2048,640]{1,2,0:T(8,128)(2,1)S(1)} %copy-done.1, f32[2048]{0:T(1024)S(1)} %add_rsqrt_fusion.1), kind=kOutput, calls=%fused_computation.37 | convolution fusion | flops 5403312128 | bytes 30416896 | tf_op jit(solution)/shard_map/dot_general | solution.py:15
  145.1 0.1 reduce-scatter.11.cloned.1.call-update
  145.1 0.1 reduce-scatter.13.cloned.1.call-start
  145.2 10.6 %convolution_convert_fusion.3 = bf16[640,2048]{1,0:T(8,128)(2,1)} fusion(bf16[2048,2048]{1,0:T(8,128)(2,1)} %get-tuple-element.24, bf16[2048,640]{0,1:T(8,128)(2,1)} %copy-done.2, f32[2048]{0:T(1024)S(1)} %add_rsqrt_fusion), kind=kOutput, calls=%fused_computation.40 | convolution fusion | flops 5373952000 | bytes 13639680 | tf_op jit(solution)/shard_map/dot_general | solution.py:15
  155.8 0.1 reduce-scatter.13.cloned.1.call-update
  155.9 0.1 reduce-scatter.7.cloned.1.call-start
  155.9 18.9 %fusion.20 = bf16[640,2048]{1,0:T(8,128)(2,1)} fusion(f32[2048,2048]{1,0:T(8,128)} %get-tuple-element.27, bf16[2048,2048]{1,0:T(8,128)(2,1)} %copy-done.12, f32[2048,2048]{1,0:T(8,128)} %fusion.43, bf16[1,2048,640]{1,2,0:T(8,128)(2,1)S(1)} %copy-done.1, f32[2048]{0:T(1024)S(1)} %add_rsqrt_fusion.1), kind=kOutput, calls=%fused_computation.36 | convolution fusion | flops 5420089344 | bytes 47194112 | tf_op jit(solution)/shard_map/dot_general | solution.py:15
  174.8 0.1 reduce-scatter.7.cloned.1.call-update
  174.9 0.1 reduce-scatter.9.cloned.1.call-start
  175.0 1.6 copy-done.4
  176.6 10.2 %convolution_convert_fusion.4 = bf16[640,2048]{1,0:T(8,128)(2,1)} fusion(bf16[2048,2048]{1,0:T(8,128)(2,1)} %get-tuple-element.25, bf16[2048,640]{0,1:T(8,128)(2,1)S(1)} %copy-done.4, f32[2048]{0:T(1024)S(1)} %add_rsqrt_fusion), kind=kOutput, calls=%fused_computation.41 | convolution fusion | flops 5373952000 | bytes 13639680 | tf_op jit(solution)/shard_map/dot_general | solution.py:15
  186.8 0.1 reduce-scatter.9.cloned.1.call-update
  186.8 0.1 reduce-scatter.15.cloned.1.call-start
  186.9 1.6 copy-done.6
  188.5 10.5 %convolution_convert_fusion.2 = bf16[2048,640]{1,0:T(8,128)(2,1)} fusion(bf16[2048,2048]{1,0:T(8,128)(2,1)} %get-tuple-element.26, bf16[2048,640]{0,1:T(8,128)(2,1)S(1)} %copy-done.6), kind=kOutput, calls=%fused_computation.39 | convolution fusion | flops 5370019840 | bytes 13631488 | tf_op jit(solution)/shard_map/dot_general | solution.py:15
  199.1 0.1 reduce-scatter.17.cloned.1.call-start
  199.1 1.6 copy-done.8
  200.8 15.6 %fusion.26 = bf16[2048,640]{1,0:T(8,128)(2,1)} fusion(f32[2048,2048]{1,0:T(8,128)} %fusion.37, f32[2048,2048]{1,0:T(8,128)} %fusion.34, bf16[1,2048,640]{2,1,0:T(8,128)(2,1)S(1)} %copy-done.8), kind=kOutput, calls=%fused_computation.38 | convolution fusion | flops 5395185664 | bytes 38797312 | tf_op jit(solution)/shard_map/dot_general | solution.py:15
  216.5 16.5 %reduce-scatter.13.cloned.1.call-done = bf16[80,2048]{1,0:T(8,128)(2,1)} async-done(((bf16[640,2048]{1,0:T(8,128)(2,1)}), bf16[80,2048]{1,0:T(8,128)(2,1)}) %reduce-scatter.13.cloned.1.call-update) | async-done | bytes 327696 | tf_op jit(solution)/shard_map/reduce_scatter | solution.py:139
  233.0 3.5 fusion.72
  236.5 39.4 %reduce-scatter.7.cloned.1.call-done = bf16[80,2048]{1,0:T(8,128)(2,1)} async-done(((bf16[640,2048]{1,0:T(8,128)(2,1)}), bf16[80,2048]{1,0:T(8,128)(2,1)}) %reduce-scatter.7.cloned.1.call-update) | async-done | bytes 327696 | tf_op jit(solution)/shard_map/reduce_scatter | solution.py:139
  275.9 43.0 %reduce-scatter.9.cloned.1.call-done = bf16[80,2048]{1,0:T(8,128)(2,1)} async-done(((bf16[640,2048]{1,0:T(8,128)(2,1)}), bf16[80,2048]{1,0:T(8,128)(2,1)}) %reduce-scatter.9.cloned.1.call-update) | async-done | bytes 327696 | tf_op jit(solution)/shard_map/reduce_scatter | solution.py:139
  318.9 4.4 fusion.68
  323.4 38.0 %reduce-scatter.15.cloned.1.call-done = bf16[256,640]{1,0:T(8,128)(2,1)} async-done(((bf16[2048,640]{1,0:T(8,128)(2,1)}), bf16[256,640]{1,0:T(8,128)(2,1)}) %reduce-scatter.15.cloned.1.call-update) | async-done | bytes 327696 | tf_op jit(solution)/shard_map/reduce_scatter | solution.py:139
  361.4 42.2 %reduce-scatter.17.cloned.1.call-done = bf16[256,640]{1,0:T(8,128)(2,1)} async-done(((bf16[2048,640]{1,0:T(8,128)(2,1)}), bf16[256,640]{1,0:T(8,128)(2,1)}) %reduce-scatter.17.cloned.1.call-update) | async-done | bytes 327696 | tf_op jit(solution)/shard_map/reduce_scatter | solution.py:139
  403.6 3.9 fusion.76
  407.5 150.9 %shard_map.178 = (bf16[2,640,2048]{2,1,0:T(8,128)(2,1)S(1)}, bf16[2,640,2048]{2,1,0:T(8,128)(2,1)S(1)}, bf16[2,2048,640]{2,1,0:T(8,128)(2,1)}) custom-call(bf16[2,80,2048]{2,1,0:T(8,128)(2,1)S(1)} %get-tuple-element.21.refs_0_, bf16[2,80,2048]{2,1,0:T(8,128)(2,1)S(1)} %get-tuple-element.18.refs_1_, bf16[2,256,640]{2,1,0:T(8,128)(2,1)S(1)} %get-tuple-element.15.refs_2_), custom_call_target="tpu_custom_call" | custom-call | tf_op jit(solution)/shard_map/pallas_call | solution.py:106
  558.5 2.7 copy.25
  561.1 2.7 copy.26
  563.8 1.1 slice-done.1
  564.9 2.4 copy.27
  (37 shorter events, 0.2 us)
Async XLA Ops:
  7.2 209.3 %reduce-scatter.11.cloned.1.call-start = ((), (), s32[]{:S(2)}) async-start(), calls=%async_computation.8 | async-start | bytes 2949120 | tf_op jit(solution)/shard_map/reduce_scatter | solution.py:139
  10.3 30.9 %copy-start = (bf16[1,2048,640]{1,2,0:T(8,128)(2,1)}, bf16[1,2048,640]{1,2,0:T(8,128)(2,1)S(1)}, u32[]{:S(2)}) copy-start(bf16[1,2048,640]{1,2,0:T(8,128)(2,1)S(1)} %copy.20) | copy-start | bytes 7864324
  10.3 2.7 copy-start.7
  50.4 12.9 %copy-start.2 = (bf16[2048,640]{0,1:T(8,128)(2,1)}, bf16[2048,640]{0,1:T(8,128)(2,1)S(1)}, u32[]{:S(2)}) copy-start(bf16[2048,640]{0,1:T(8,128)(2,1)S(1)} %get-tuple-element.29) | copy-start | bytes 7864324
  102.4 10.0 %copy-start.3 = (bf16[2048,640]{0,1:T(8,128)(2,1)S(1)}, bf16[2048,640]{0,1:T(8,128)(2,1)}, u32[]{:S(2)}) copy-start(bf16[2048,640]{0,1:T(8,128)(2,1)} %copy-done.2) | copy-start | bytes 7864324
  102.4 10.0 %copy-start.13 = (bf16[2048,2048]{1,0:T(8,128)(2,1)S(1)}, bf16[2048,2048]{1,0:T(8,128)(2,1)}, u32[]{:S(2)}) copy-start(bf16[2048,2048]{1,0:T(8,128)(2,1)} %get-tuple-element.25) | copy-start | bytes 25165828
  102.4 21.2 %slice-start.2 = ((s8[5242880]{0:T(1024)(128)(4,1)}), s8[4194304]{0:T(1024)(128)(4,1)S(1)}, s32[]{:S(2)}) async-start(s8[5242880]{0:T(1024)(128)(4,1)} %bitcast.80), calls=%async_computation.14 | async-start | bytes 8388608
  112.4 11.2 %slice-start.3 = ((s8[5242880]{0:T(1024)(128)(4,1)}), s8[1048576]{0:T(1024)(128)(4,1)S(1)}, s32[]{:S(2)}) async-start(s8[5242880]{0:T(1024)(128)(4,1)} %bitcast.80), calls=%async_computation.15 | async-start | bytes 2097152
  122.1 1.5 copy-start.5
  123.6 10.3 %copy-start.1 = (bf16[1,2048,640]{1,2,0:T(8,128)(2,1)S(1)}, bf16[1,2048,640]{1,2,0:T(8,128)(2,1)}, u32[]{:S(2)}) copy-start(bf16[1,2048,640]{1,2,0:T(8,128)(2,1)} %copy-done) | copy-start | bytes 7864324
  130.7 3.2 copy-start.12
  145.1 87.9 %reduce-scatter.13.cloned.1.call-start = ((), (), s32[]{:S(2)}) async-start(), calls=%async_computation.9 | async-start | bytes 2949120 | tf_op jit(solution)/shard_map/reduce_scatter | solution.py:139
  155.9 120.0 %reduce-scatter.7.cloned.1.call-start = ((), (), s32[]{:S(2)}) async-start(), calls=%async_computation.6 | async-start | bytes 2949120 | tf_op jit(solution)/shard_map/reduce_scatter | solution.py:139
  174.8 1.7 copy-start.4
  174.9 144.0 %reduce-scatter.9.cloned.1.call-start = ((), (), s32[]{:S(2)}) async-start(), calls=%async_computation.7 | async-start | bytes 2949120 | tf_op jit(solution)/shard_map/reduce_scatter | solution.py:139
  186.8 1.7 copy-start.6
  186.8 174.6 %reduce-scatter.15.cloned.1.call-start = ((), (), s32[]{:S(2)}) async-start(), calls=%async_computation.10 | async-start | bytes 2949120 | tf_op jit(solution)/shard_map/reduce_scatter | solution.py:139
  199.0 1.7 copy-start.8
  199.1 204.5 %reduce-scatter.17.cloned.1.call-start = ((), (), s32[]{:S(2)}) async-start(), calls=%async_computation.11 | async-start | bytes 2949120 | tf_op jit(solution)/shard_map/reduce_scatter | solution.py:139
  216.4 16.6 %copy-start.9 = (f32[2,80,2048]{2,1,0:T(8,128)S(1)}, f32[2,80,2048]{2,1,0:T(8,128)}, u32[]{:S(2)}) copy-start(f32[2,80,2048]{2,1,0:T(8,128)} %param.20) | copy-start | bytes 3932164
  216.4 16.6 %copy-start.10 = (f32[2,80,2048]{2,1,0:T(8,128)S(1)}, f32[2,80,2048]{2,1,0:T(8,128)}, u32[]{:S(2)}) copy-start(f32[2,80,2048]{2,1,0:T(8,128)} %param.17) | copy-start | bytes 3932164
  318.9 84.6 %copy-start.11 = (f32[2,256,640]{2,1,0:T(8,128)S(1)}, f32[2,256,640]{2,1,0:T(8,128)}, u32[]{:S(2)}) copy-start(f32[2,256,640]{2,1,0:T(8,128)} %param.21) | copy-start | bytes 3932164
  558.4 5.3 slice-start
  561.1 3.8 slice-start.1
Sparse Core Ops, SparseCore 0:
  145.2 44.4 reduce-scatter.10
  192.7 40.2 reduce-scatter.12
  235.9 39.9 reduce-scatter.6
  278.7 40.2 reduce-scatter.8
  321.1 40.2 reduce-scatter.14
  363.6 39.9 reduce-scatter.16

commit v2 on v0

v2 whole, which is shorter than its diff:
```python
import functools

import jax
import jax.numpy as jnp
from jax import lax
from jax.experimental import pallas as pl
from jax.experimental.pallas import tpu as pltpu
from jax.sharding import PartitionSpec as P

MESH = pl.DeviceIdType.MESH
F32, BF16 = jnp.float32, jnp.bfloat16
TILE = 256
SLOTS = 4
ANY = pl.BlockSpec(memory_space=pl.ANY)


def dot(a, b, ca, cb):
    return lax.dot_general(a, b, (((ca,), (cb,)), ((), ())), preferred_element_type=F32)


def normed(h):
    wide = h.astype(F32)
    scale = lax.rsqrt(jnp.mean(wide**2, -1, keepdims=True) + 1e-6)
    return (wide * scale).astype(BF16)


def kernel(n, *refs):
    x, dy, wg, wu, wd, mg, mu, md, vg, vu, vd = refs[:11]
    og, ou, od, omg, omu, omd, ovg, ovu, ovd = refs[11:20]
    (a, a_t, d, d_t, h, acc, dgu, hid, wgu, wdn, own_gu, own_d, land, land_d, g_gu, g_d,
     m_gu, v_gu, w_gu, n_gu, m_d, v_d, w_d, n_d,
     rs_send, rs_recv, dn_send, dn_recv, ag_send, ag_recv, own_sem, load_sem, tile_sem, adam_sem, out_sem) = refs[20:]
    tokens, width = h.shape
    tiles = wg.shape[2] // TILE
    chains = 2 * tiles
    rows, rows_d = m_gu.shape[1], m_d.shape[0]
    half = rows_d // 2
    quarter = half // 2
    supers = tiles // 2
    block = tokens // 2
    me = lax.axis_index("dp")
    right, left = lax.rem(me + 1, n), lax.rem(me + n - 1, n)

    barrier = pltpu.get_barrier_semaphore()
    for neighbour in (left, right):
        pl.semaphore_signal(barrier, inc=1, device_id={"dp": neighbour}, device_id_type=MESH)
    def towards(way):
        return {"dp": right if way == 0 else left}

    hops = (n // 2, n - 1 - n // 2)

    def count(part, way):
        return hops[0] if part == way else hops[1]

    def owner_at(step, part, way):
        far = count(part, way) - step
        return lax.rem(me + far, n) if way == 0 else lax.rem(me + n - far, n)

    def place(step, part, way):
        return step if part == way else hops[0] + step

    def ring_copy(ring, c, step, part, way):
        own, land, send_sem, recv_sem = ring
        src = own(c, part, owner_at(0, part, way)) if step == 0 else land.at[c, part, place(step - 1, part, way)]
        here = place(step, part, way)
        return pltpu.make_async_remote_copy(
            src_ref=src, dst_ref=land.at[c, part, here], send_sem=send_sem.at[c, part, way], recv_sem=recv_sem.at[c, part, here],
            device_id=towards(way), device_id_type=MESH,
        )

    def ring_start(ring, c):
        for part in range(2):
            for way in range(2):
                ring_copy(ring, c, 0, part, way).start()

    def ring_step(ring, c, step, finish):
        own, land = ring[:2]
        for part in range(2):
            for way in range(2):
                last = count(part, way)
                if step > last:
                    continue
                ring_copy(ring, c, step - 1, part, way).wait_recv()
                ring_copy(ring, c, step - 1, part, way).wait_send()
                if step < last:
                    at = land.at[c, part, place(step - 1, part, way)]
                    at[...] = (at[...].astype(F32) + own(c, part, owner_at(step, part, way))[...].astype(F32)).astype(BF16)
                    ring_copy(ring, c, step, part, way).start()
        if step == hops[0]:
            for part in range(2):
                total = own(c, part, me)[...].astype(F32)
                for way in range(2):
                    total += land[c, part, place(count(part, way) - 1, part, way)].astype(F32)
                finish(c, part, total.astype(BF16))

    def strips(i):
        t = lax.rem(i, tiles)
        first = lax.rem(t, supers) * 2 * rows_d + (t // supers) * half
        return [pl.ds(pl.multiple_of(first + e * rows_d, half), half) for e in range(2)]

    def tile_loads(i):
        layer, slot = lax.rem(i // tiles, 2), lax.rem(i, 2)
        copies = []
        for e, strip in enumerate(strips(i)):
            here = pl.ds(e * half, half)
            copies += [
                pltpu.make_async_copy(wg.at[layer, :, strip], wgu.at[slot, :, here], tile_sem.at[slot, e, 0]),
                pltpu.make_async_copy(wu.at[layer, :, strip], wgu.at[slot, :, pl.ds(TILE + e * half, half)], tile_sem.at[slot, e, 1]),
                pltpu.make_async_copy(wd.at[layer, strip, :], wdn.at[slot, here, :], tile_sem.at[slot, e, 2]),
            ]
        return copies

    def adam_loads(layer):
        mine = pl.ds(pl.multiple_of(me * rows, 16), rows)
        mine_d = pl.ds(pl.multiple_of(me * rows_d, 16), rows_d)
        pairs = (
            (mg.at[layer], m_gu.at[0]), (mu.at[layer], m_gu.at[1]), (vg.at[layer], v_gu.at[0]), (vu.at[layer], v_gu.at[1]),
            (wg.at[layer, mine, :], w_gu.at[0]), (wu.at[layer, mine, :], w_gu.at[1]),
            (md.at[layer], m_d), (vd.at[layer], v_d), (wd.at[layer, mine_d, :], w_d),
        )
        return [pltpu.make_async_copy(s, t, adam_sem.at[k]) for k, (s, t) in enumerate(pairs)]

    def adam_stores(layer, which):
        gu = ((m_gu.at[0], omg.at[layer]), (m_gu.at[1], omu.at[layer]), (v_gu.at[0], ovg.at[layer]), (v_gu.at[1], ovu.at[layer]))
        down = ((m_d, omd.at[layer]), (v_d, ovd.at[layer]))
        pairs, first = (gu, 0) if which == "gu" else (down, 4)
        return [pltpu.make_async_copy(s, t, out_sem.at[first + k]) for k, (s, t) in enumerate(pairs)]

    def tile_own(c, part, owner):
        return own_gu.at[lax.rem(c, SLOTS), part, pl.ds(pl.multiple_of(owner * rows, 16), rows), :]

    def tile_finish(c, part, total):
        for e, strip in enumerate(strips(c)):
            g_gu[c // tiles, part, :, strip] = total[:, e * half : (e + 1) * half]

    tile_ring = (tile_own, land, rs_send, rs_recv)

    def tile_step(c, step):
        @pl.when((c >= 0) & (c < chains))
        def _():
            ring_step(tile_ring, c, step, tile_finish)

    def down_rows(k, part, owner):
        return pl.ds(pl.multiple_of(owner * rows_d + lax.rem(k, 2) * half + part * quarter, 16), quarter)

    def down_own(k, part, owner):
        return own_d.at[k // 2, down_rows(k, part, owner), :]

    def down_finish(k, part, total):
        g_d[k // 2, down_rows(k, part, 0), :] = total

    down_ring = (down_own, land_d, dn_send, dn_recv)

    def down_steps(i, some):
        for step in some:
            ago = i - supers + 1 - step
            k = ago // supers

            @pl.when((lax.rem(ago, supers) == 0) & (ago >= 0) & (k < 3))
            def _():
                ring_step(down_ring, k, step, down_finish)

    def piece(ref, k, layer, owner, way):
        if k < 2:
            w = ref.shape[-1] // 2
            if layer is None:
                return ref.at[:, pl.ds(way * w, w)]
            return ref.at[layer, pl.ds(pl.multiple_of(owner * rows, 16), rows), pl.ds(way * w, w)]
        if layer is None:
            return ref.at[pl.ds(way * half, half), :]
        return ref.at[layer, pl.ds(pl.multiple_of(owner * rows_d + way * half, 16), half), :]

    def fresh(k, number):
        return (n_gu.at[number, 0], n_gu.at[number, 1], n_d.at[number])[k]

    def ag_copy(number, k, way, hop):
        layer, out = 1 - number, (og, ou, od)[k]
        owner = lax.rem(me + n - hop, n) if way == 0 else lax.rem(me + hop, n)
        dst = piece(out, k, layer, owner, way)
        src = piece(fresh(k, number), k, None, 0, way) if hop == 0 else dst
        item = 3 * number + k
        return pltpu.make_async_remote_copy(
            src_ref=src, dst_ref=dst, send_sem=ag_send.at[item, way], recv_sem=ag_recv.at[item, way, hop],
            device_id=towards(way), device_id_type=MESH,
        )

    def own_copy(number, k):
        layer, out = 1 - number, (og, ou, od)[k]
        count = (rows, rows, rows_d)[k]
        dst = out.at[layer, pl.ds(pl.multiple_of(me * count, 16), count), :]
        return pltpu.make_async_copy(fresh(k, number), dst, own_sem.at[3 * number + k])

    def ag_start(number, k):
        for way in range(2):
            ag_copy(number, k, way, 0).start()
        own_copy(number, k).start()

    def ag_hop(number, k, hop):
        for way in range(2):
            ag_copy(number, k, way, hop - 1).wait_recv()
            ag_copy(number, k, way, hop - 1).wait_send()
            if hop < n - 1:
                ag_copy(number, k, way, hop).start()

    def adamw(w, m, v, g):
        w, g = w[...].astype(F32), g.astype(F32)
        new_m = 0.9 * m[...] + 0.1 * g
        new_v = 0.95 * v[...] + 0.05 * g * g
        m[...] = new_m
        v[...] = new_v
        return (w - 0.02 * (new_m * lax.rsqrt(new_v + 1e-8) + 0.1 * w)).astype(BF16)

    def adam_gu(number):
        for k in range(2):
            n_gu[number, k] = adamw(w_gu.at[k], m_gu.at[k], v_gu.at[k], g_gu[number, k])
        for c in adam_stores(1 - number, "gu"):
            c.start()

    def adam_down(number):
        n_d[number] = adamw(w_d, m_d, v_d, g_d[number])
        for c in adam_stores(1 - number, "down"):
            c.start()

    def turn(src, dst):
        for at in range(0, tokens, TILE):
            dst[:, pl.ds(at, TILE)] = src[pl.ds(at, TILE), :].T

    def forward(i, part):
        slot = lax.rem(i, 2)
        at = pl.ds(part * block, block)
        both = dot(a[at, :], wgu[slot], 1, 0)
        gate, up = both[:, :TILE], both[:, TILE:]
        silu = gate * (0.5 * jnp.tanh(0.5 * gate) + 0.5)
        acc[at, :] += dot((silu * up).astype(BF16), wdn[slot], 1, 0)

    def forward_and_back(i, part, with_da):
        slot = lax.rem(i, 2)
        at = pl.ds(part * block, block)
        both = dot(a[at, :], wgu[slot], 1, 0)
        gate, up = both[:, :TILE], both[:, TILE:]
        dh = dot(d[at, :], wdn[slot], 1, 1).astype(BF16).astype(F32)
        s = 0.5 * jnp.tanh(0.5 * gate) + 0.5
        silu = gate * s
        hid[at, :] = (silu * up).astype(BF16)
        dgu[at, pl.ds(0, TILE)] = (dh * up * (s + silu * (1 - s))).astype(BF16)
        dgu[at, pl.ds(TILE, TILE)] = (dh * silu).astype(BF16)
        if with_da:
            acc[at, :] += dot(dgu[at, :], wgu[slot], 1, 1)

    def weights_back(i):
        both = dot(a_t[...], dgu[...], 1, 0)
        slot = lax.rem(i, SLOTS)
        own_gu[slot, 0] = both[:, :TILE].astype(BF16)
        own_gu[slot, 1] = both[:, TILE:].astype(BF16)

    def down_back(i):
        grad = dot(d_t[...], hid[...], 1, 0).T.astype(BF16)
        for e, strip in enumerate(strips(i)):
            own_d[i // tiles, strip, :] = grad[e * half : (e + 1) * half]

    def steps(i, part):
        for behind, step in (((2, 2),), ((1, 1),), ((3, 4),), ((2, 3),))[part]:
            tile_step(i - behind, step)

    def tile_in(i):
        @pl.when(i + 1 < 3 * tiles)
        def _():
            for c in tile_loads(i + 1):
                c.start()
        for c in tile_loads(i):
            c.wait()

    def one_tile(i, with_da):
        tile_in(i + tiles)
        forward_and_back(i, 0, with_da)
        steps(i, 0)
        forward_and_back(i, 1, with_da)
        steps(i, 1)
        weights_back(i)
        ring_start(tile_ring, i)
        if with_da:
            @pl.when(i == 0)
            def _():
                turn(d, d_t)
        steps(i, 2)
        down_back(i)
        steps(i, 3)
        down_steps(i, range(1, hops[0] + 1))

        @pl.when(lax.rem(i, supers) == supers - 1)
        def _():
            ring_start(down_ring, i // supers)

    def blocks(body):
        @pl.loop(0, tokens // TILE)
        def _(b):
            body(pl.ds(pl.multiple_of(b * TILE, TILE), TILE))

    loads = [pltpu.make_async_copy(s, t, load_sem.at[k]) for k, (s, t) in enumerate(((x, h), (dy, d), (x, a)))]
    loads[0].start()
    for c in tile_loads(0):
        c.start()
    loads[1].start()
    for c in adam_loads(1):
        c.start()
    loads[0].wait()

    def first(at):
        a[at, :] = normed(h[at, :])
        acc[at, :] = jnp.zeros((TILE, width), F32)

    blocks(first)

    @pl.loop(0, tiles)
    def _(i):
        tile_in(i)
        forward(i, 0)
        forward(i, 1)

    def second(at):
        state = (h[at, :].astype(F32) + acc[at, :].astype(BF16).astype(F32)).astype(BF16)
        h[at, :] = state
        a[at, :] = normed(state)
        acc[at, :] = jnp.zeros((TILE, width), F32)

    pl.semaphore_wait(barrier, 2)
    blocks(second)
    turn(a, a_t)
    loads[1].wait()

    @pl.loop(0, tiles)
    def _(i):
        one_tile(i, True)

    loads[2].start()

    def between(at):
        wide = h[at, :].astype(F32)
        da = acc[at, :].astype(BF16).astype(F32)
        scale = lax.rsqrt(jnp.mean(wide * wide, -1, keepdims=True) + 1e-6)
        mean = jnp.mean(da * wide, -1, keepdims=True)
        dn = (da * scale - wide * (scale * scale * scale * mean)).astype(BF16).astype(F32)
        d[at, :] = (d[at, :].astype(F32) + dn).astype(BF16)

    blocks(between)
    turn(d, d_t)
    loads[2].wait()

    def again(at):
        a[at, :] = normed(a[at, :])

    blocks(again)
    turn(a, a_t)

    @pl.loop(tiles, chains)
    def _(i):
        one_tile(i, False)

    for c in adam_loads(1):
        c.wait()
    adam_gu(0)
    adam_down(0)
    for k in range(3):
        ag_start(0, k)

    @pl.loop(chains, chains + 3)
    def _(i):
        for part in range(4):
            steps(i, part)

    for which in ("gu", "down"):
        for c in adam_stores(1, which):
            c.wait()
    for c in adam_loads(0):
        c.start()
    for hop in range(1, n):
        for k in range(3):
            ag_hop(0, k, hop)
        if hop == n - 3:
            for c in adam_loads(0):
                c.wait()
            adam_gu(1)
        if hop == n - 2:
            ag_start(1, 0)
            ag_start(1, 1)
        if hop <= hops[0]:
            ring_step(down_ring, 3, hop, down_finish)
    adam_down(1)
    ag_start(1, 2)
    for hop in range(1, n):
        for k in range(3):
            ag_hop(1, k, hop)
    for which in ("gu", "down"):
        for c in adam_stores(0, which):
            c.wait()
    for number in range(2):
        for k in range(3):
            own_copy(number, k).wait()


def hand_out(*refs):
    ins, outs, held, (in_sem, out_sem) = refs[:9], refs[9:18], refs[18:27], refs[27:]
    pieces = [(k, layer) for layer in range(ins[0].shape[0]) for k in range(9)]
    reads = [pltpu.make_async_copy(ins[k].at[l], held[k].at[l], in_sem.at[k, l]) for k, l in pieces]
    writes = [pltpu.make_async_copy(held[k].at[l], outs[k].at[l], out_sem.at[k, l]) for k, l in pieces]
    for c in reads:
        c.start()
    for r, w in zip(reads, writes, strict=True):
        r.wait()
        w.start()
    for c in writes:
        c.wait()


def solution(mesh):
    n = mesh.shape["dp"]

    def step(x, dy, wg, wu, wd, mg, mu, md, vg, vu, vd):
        x, dy = x[0], dy[0]
        tokens, width = x.shape
        ff = wg.shape[2]
        rows, rows_d = mg.shape[1], md.shape[1]
        tiles = ff // TILE
        shape = jax.ShapeDtypeStruct
        sem, vm = pltpu.SemaphoreType.DMA, pltpu.VMEM
        hop = n - 1
        shapes = tuple(shape(t.shape, t.dtype) for t in (wg, wu, wd, mg, mu, md, vg, vu, vd))
        outs = pl.pallas_call(
            functools.partial(kernel, n),
            out_shape=shapes,
            in_specs=[ANY] * 11,
            out_specs=(ANY,) * 9,
            scratch_shapes=[
                vm((tokens, width), BF16), vm((width, tokens), BF16), vm((tokens, width), BF16), vm((width, tokens), BF16),
                vm((tokens, width), BF16), vm((tokens, width), F32), vm((tokens, 2 * TILE), BF16), vm((tokens, TILE), BF16),
                vm((2, width, 2 * TILE), BF16), vm((2, TILE, width), BF16),
                vm((SLOTS, 2, width, TILE), BF16), vm((2, ff, width), BF16),
                vm((2 * tiles, 2, hop, rows, TILE), BF16), vm((4, 2, hop, rows_d // 4, width), BF16),
                vm((2, 2, rows, ff), BF16), vm((2, rows_d, width), BF16),
                vm((2, rows, ff), F32), vm((2, rows, ff), F32), vm((2, rows, ff), BF16), vm((2, 2, rows, ff), BF16),
                vm((rows_d, width), F32), vm((rows_d, width), F32), vm((rows_d, width), BF16), vm((2, rows_d, width), BF16),
                sem((2 * tiles, 2, 2)), sem((2 * tiles, 2, hop)), sem((4, 2, 2)), sem((4, 2, hop)),
                sem((6, 2)), sem((6, 2, hop)), sem((6,)), sem((3,)), sem((2, 2, 3)), sem((9,)), sem((6,)),
            ],
            compiler_params=pltpu.CompilerParams(collective_id=0, has_side_effects=True, vmem_limit_bytes=67_000_000),
        )(x, dy, wg, wu, wd, mg, mu, md, vg, vu, vd)
        return pl.pallas_call(
            hand_out,
            out_shape=shapes,
            in_specs=[ANY] * 9,
            out_specs=(ANY,) * 9,
            scratch_shapes=[*(vm(t.shape, t.dtype) for t in shapes), sem((9, 2)), sem((9, 2))],
            compiler_params=pltpu.CompilerParams(vmem_limit_bytes=67_000_000),
        )(*outs)

    seq, whole, rows = P(("rep", "dp")), P(), P(None, "dp")
    out_w, out_m = P("rep"), P("rep", "dp")
    return jax.shard_map(
        step,
        mesh=mesh,
        in_specs=(seq, seq, *[whole] * 3, *[rows] * 6),
        out_specs=(*[out_w] * 3, *[out_m] * 6),
        check_vma=False,
    )
```

time: 696 us -> 382 us (0.55); the launches traced: 686 us -> 382 us
  waiting for transfers between devices: 413 us -> 0 us
  Pallas kernels: 0 us -> 381 us
  matrix products: 182 us -> 0 us
  other arithmetic: 46.8 us -> 0 us
  local copies, waits for them, and re-layouts: 27.3 us -> 0 us
  between operations: 15.2 us -> 0.81 us
    pallas_call x0 -> x2, Pallas kernels: none -> 381 us  [the longest x1 364 us: step(): pl.pallas_call(functools.partial(kernel, n), out_shape=shapes, in_specs=[...]
    unnamed x15 -> x0, waiting for transfers between devices: 233 us -> none
    dot_general x15 -> x0, matrix products: 182 us -> none  [the longest x5 64.8 us: layer(): up = jnp.dot(a, w['w_up'], preferred_element_type=jnp.float32)]
    reshape x3 -> x0, waiting for transfers between devices: 181 us -> none  [step(): t.reshape(-1, *t.shape[2:])]
    unnamed x49 -> x0, local copies, waits for them, and re-layouts: 26.7 us -> none
    unnamed x4 -> x0, other arithmetic: 26.2 us -> none
    reshape x3 -> x0, other arithmetic: 11.3 us -> none  [step(): t.reshape(-1, *t.shape[2:])]
  transfers between devices with their start and end apart: 9 -> 0, of which waited for: 7 -> 0; matrix products, arithmetic and copies ran while one was open for 22% -> 0% of each run, Pallas kernels for 0% -> 0%
where the time goes in v2:
time: 382 us
  Pallas kernels  381 us (100%)
    pallas_call x1, Pallas kernels, step(): pl.pallas_call(functools.partial(kernel, n), out_shape=shapes, in_specs=[...  364 us
    pallas_call x1, Pallas kernels, step(): pl.pallas_call(hand_out, out_shape=shapes, in_specs=[ANY] * 9, out_specs=...  16.5 us

profile of v2, /device:TPU:30, one launch (start us, length us, event | category | flops | bytes accessed | tf_op | source)
XLA Modules:
  0.0 381.8 jit_solution(8669107330885075703)
XLA Ops:
  0.6 364.5 %shard_map.178 = (bf16[2,640,2048]{2,1,0:T(8,128)(2,1)}, bf16[2,640,2048]{2,1,0:T(8,128)(2,1)}, bf16[2,2048,640]{2,1,0:T(8,128)(2,1)}, f32[2,80,2048]{2,1,0:T(8,...) custom-call(bf16[2048,640]{1,0:T(8,128)(2,1)} %bitcast.2, ...), custom_call_target="tpu_custom_call" | custom-call | tf_op jit(solution)/shard_map/pallas_call | solution.py:428
  365.1 16.5 %shard_map.179 = (bf16[2,640,2048]{2,1,0:T(8,128)(2,1)}, bf16[2,640,2048]{2,1,0:T(8,128)(2,1)}, bf16[2,2048,640]{2,1,0:T(8,128)(2,1)}, f32[2,80,2048]{2,1,0:T(8,...) custom-call(bf16[2,640,2048]{2,1,0:T(8,128)(2,1)} %get-tuple-element, ...), custom_call_target="tpu_custom_call" | custom-call | tf_op jit(solution)/shard_map/pallas_call | solution.py:447

commit v3 on v2

--- a/solution.py
+++ b/solution.py
@@ -363,17 +363,16 @@
     for k in range(3):
         ag_start(0, k)
 
-    @pl.loop(chains, chains + 3)
-    def _(i):
-        for part in range(4):
-            steps(i, part)
-
-    for which in ("gu", "down"):
-        for c in adam_stores(1, which):
-            c.wait()
-    for c in adam_loads(0):
-        c.start()
     for hop in range(1, n):
+        if hop < hops[0]:
+            for part in range(4):
+                steps(me * 0 + chains + hop - 1, part)
+        if hop == hops[0]:
+            for which in ("gu", "down"):
+                for c in adam_stores(1, which):
+                    c.wait()
+            for c in adam_loads(0):
+                c.start()
         for k in range(3):
             ag_hop(0, k, hop)
         if hop == n - 3:

time: 382 us -> 379 us (level)
  no operation moved by 1% of the time
where the time goes in v3:
time: 379 us
  Pallas kernels  378 us (100%)
    pallas_call x1, Pallas kernels, step(): pl.pallas_call(functools.partial(kernel, n), out_shape=shapes, in_specs=[...  362 us
    pallas_call x1, Pallas kernels, step(): pl.pallas_call(hand_out, out_shape=shapes, in_specs=[ANY] * 9, out_specs=...  16.5 us

profile of v3, /device:TPU:30, one launch (start us, length us, event | category | flops | bytes accessed | tf_op | source)
XLA Modules:
  0.0 379.0 jit_solution(6141157698053262342)
XLA Ops:
  0.6 361.7 %shard_map.178 = (bf16[2,640,2048]{2,1,0:T(8,128)(2,1)}, bf16[2,640,2048]{2,1,0:T(8,128)(2,1)}, bf16[2,2048,640]{2,1,0:T(8,128)(2,1)}, f32[2,80,2048]{2,1,0:T(8,...) custom-call(bf16[2048,640]{1,0:T(8,128)(2,1)} %bitcast.2, ...), custom_call_target="tpu_custom_call" | custom-call | tf_op jit(solution)/shard_map/pallas_call | solution.py:427
  362.3 16.5 %shard_map.179 = (bf16[2,640,2048]{2,1,0:T(8,128)(2,1)}, bf16[2,640,2048]{2,1,0:T(8,128)(2,1)}, bf16[2,2048,640]{2,1,0:T(8,128)(2,1)}, f32[2,80,2048]{2,1,0:T(8,...) custom-call(bf16[2,640,2048]{2,1,0:T(8,128)(2,1)} %get-tuple-element, ...), custom_call_target="tpu_custom_call" | custom-call | tf_op jit(solution)/shard_map/pallas_call | solution.py:446
